TPU v7x, 32 devices: a whole 2x2x4 slice. The times are simulated.
32 devices in a mesh: row: 4 (over y, core), col: 8 (over z, x).
Axes of the slice: x: 2, y: 2, z: 4, core: 2. Of those that a mesh axis runs over, the one named last changes fastest.
Arguments:
- amplitudes: float32 [48, 256, 1024], P('col', None, 'row'), may hold values from -6 to 6
- interaction: float32 [8192, 8192], P('row', 'col'), may hold values from -0.5 to 0.5, as said below
- tile_counts: int32 [8], replicated, may hold values from 2 to 6, as said below
- tile_block: int32 [48], replicated, may hold values from -1 to 31, as said below
- recouple_sign: int32 [48], replicated, may hold values from 0 to 1
- orbit_perm: int32 [48, 256], replicated, may hold values from 0 to 255, each once within a row
- particle_energy: float32 [48, 256], P('col'), may hold values from -2 to 2
Outputs:
- sigma: float32 [48, 256, 1024], P('col', None, 'row')
Inputs may be any that keep to these rules, and one draw needn't show every extreme that they name: Owner c holds its live tiles in its first tile_counts[c] slots; the counts sum to 32, and some owner holds 6. `tile_block`: live slots map one to one onto the 32 cross-channel tiles, and slots that are not live hold -1; two live tiles of one owner never lie in the same aligned group of 4 cross-channel tiles. interaction equals its transpose.
All inputs are finite; a program needn't handle non-finite values.
Results may differ from a plain program's by a relative error of at most 0.000061.
Values sent between devices are 32-bit elements; how exact they have to be, the bound alone decides.
No kernel may reach another device: no remote copies, remote signals or barrier semaphores. Data moves between devices by JAX's collectives and lax.ppermute only.
A program may use at most 128 MiB of HBM per device.

v0:
```python
import jax
import jax.numpy as jnp
from jax import lax
from jax.sharding import PartitionSpec as P


def tile_recouple(tiles, phases, orders):
    moved = jax.vmap(lambda single, ordering: jnp.take(single, ordering, axis=0))(tiles, orders)
    return moved * phases[:, None, None]


def local(
    amplitudes, interaction, tile_counts, tile_block, recouple_sign, orbit_perm, particle_energy
):
    column_index = lax.axis_index("col")
    row_index = lax.axis_index("row")
    column_count = lax.axis_size("col")
    slots, tile_rows, narrow_cols = amplitudes.shape
    row_blocks = interaction.shape[0] // tile_rows
    col_blocks = interaction.shape[1] // tile_rows
    tile_total = tile_block.shape[0]
    slot_ids = jnp.arange(slots, dtype=jnp.int32)
    is_live = slot_ids < jnp.take(tile_counts, column_index)
    live_mask = is_live.astype(jnp.float32)[:, None, None]
    own_block = jnp.where(
        is_live, lax.dynamic_slice_in_dim(tile_block, column_index * slots, slots), -1
    )
    all_phases = (1 - 2 * recouple_sign).astype(jnp.float32)
    own_phases = lax.dynamic_slice_in_dim(all_phases, column_index * slots, slots)
    own_orders = lax.dynamic_slice_in_dim(orbit_perm, column_index * slots, slots, 0)
    diagonal = particle_energy[:, :, None] * amplitudes
    tile_ids = jnp.arange(tile_total, dtype=jnp.int32)
    peer_ids = jnp.arange(column_count, dtype=jnp.int32)

    def tiles_of(blocks):
        matches = tile_block[None, :] == blocks[:, None]
        return jnp.sum(jnp.where(matches, tile_ids[None, :], 0), axis=1)

    target_col = own_block // col_blocks
    my_blocks = column_index * col_blocks + jnp.arange(col_blocks, dtype=jnp.int32)
    block_tiles = tiles_of(my_blocks)
    widened = lax.all_gather(amplitudes, "row", axis=2, tiled=True)
    widened = tile_recouple(widened, own_phases, own_orders)
    group_blocks = row_index * row_blocks + jnp.arange(row_blocks, dtype=jnp.int32)
    group_tiles = tiles_of(group_blocks)
    is_owned = group_tiles // slots == column_index
    placed = (
        jnp.take(widened, group_tiles % slots, axis=0) * is_owned.astype(jnp.float32)[:, None, None]
    )
    crossed = lax.psum(placed.reshape(row_blocks * tile_rows, widened.shape[2]), "col")
    partial_cols = lax.dot_general(
        interaction,
        crossed,
        (((0,), (0,)), ((), ())),
        precision=lax.Precision.HIGHEST,
        preferred_element_type=jnp.float32,
    )
    own_part = lax.psum_scatter(partial_cols, "row", scatter_dimension=1, tiled=True)
    blocks_here = own_part.reshape(col_blocks, tile_rows, narrow_cols)
    block_inverse = jnp.argsort(jnp.take(orbit_perm, block_tiles, axis=0), axis=1)
    blocks_here = tile_recouple(blocks_here, jnp.take(all_phases, block_tiles), block_inverse)
    block_owner = block_tiles // slots
    choose_mask = block_owner[None, :] == peer_ids[:, None]
    choose_block = jnp.sum(
        jnp.where(choose_mask, jnp.arange(col_blocks, dtype=jnp.int32)[None, :], 0), axis=1
    )
    choose_weight = jnp.max(choose_mask.astype(jnp.float32), axis=1)
    outgoing = jnp.take(blocks_here, choose_block, axis=0) * choose_weight[:, None, None]
    arrived = lax.all_to_all(outgoing, "col", split_axis=0, concat_axis=0, tiled=True)
    returned = jnp.take(arrived, jnp.clip(target_col, 0, column_count - 1), axis=0)
    return (returned + diagonal) * live_mask


def solution(mesh):
    placed = (P("col", None, "row"), P("row", "col"), P(), P(), P(), P(), P("col", None))
    return jax.shard_map(
        local, mesh=mesh, in_specs=placed, out_specs=P("col", None, "row"), check_vma=False
    )
```

profile of v0, /device:TPU:0, one launch (start us, length us, event | category | flops | bytes accessed | tf_op | source)
XLA Modules:
  0.0 530.0 jit_solution(5683541795034638029)
XLA Ops:
  7.4 0.0 all-gather.2.cloned.1.call-start
  7.4 0.7 all-gather.2.cloned.1.call-update
  8.1 0.0 all-reduce.2.cloned.1.call-start
  8.1 0.7 subtract_convert_fusion
  8.8 0.1 dynamic_slice.11
  8.9 0.7 bitcast_or_fusion
  9.6 0.8 select_reduce_fusion
  10.5 0.1 broadcast_bitcast_fusion
  10.6 0.1 broadcast_in_dim.144
  10.7 0.7 compare_and_fusion
  11.4 47.4 %all-gather.2.cloned.1.call-done = f32[6,256,1024]{2,1,0:T(8,128)} async-done(((f32[6,256,256]{2,1,0:T(8,128)}), f32[6,256,1024]{2,1,0:T(8,128)}) %all-gather.2.cloned.1.call-update) | async-done | bytes 6291472 | tf_op jit(solution)/shard_map/all_gather | solution.py:42
  58.8 30.4 %gather_fusion.5 = f32[1536,1024]{1,0:T(8,128)} fusion(f32[6,256,1024]{2,1,0:T(8,128)} %all-gather.2.cloned.1.call-done, s32[1536]{0:T(1024)S(1)} %reshape.217), kind=kCustom, calls=%fused_computation.5 | custom fusion | bytes 12595200 | tf_op jit(solution)/shard_map/vmap(jit(_take))/gather | solution.py:8
  89.3 4.9 select_multiply_fusion
  94.2 7.1 %gather_fusion.1 = f32[8,256,1024]{2,1,0:T(8,128)} fusion(f32[6,256,1024]{2,1,0:T(8,128)} %select_multiply_fusion, s32[1024]{0:T(1024)S(1)} %pad_clamp_fusion.2), kind=kCustom, calls=%fused_computation.1 | custom fusion | bytes 16777248 | tf_op jit(solution)/shard_map/jit(_take)/gather | solution.py:48
  101.2 5.8 %fusion = f32[2048,1024]{1,0:T(8,128)} fusion(f32[8,256,1024]{2,1,0:T(8,128)} %gather_fusion.1, f32[2048]{0:T(1024)S(1)} %bitcast.44, pred[2048]{0:T(1024)(128)(4,1)S(1)} %broadcast_in_dim.145), kind=kLoop, calls=%fused_computation.8 | loop fusion | flops 4194304 | bytes 16787456 | tf_op jit(solution)/shard_map/mul | solution.py:48
  107.1 0.0 all-reduce.2.cloned.1.call-update
  107.1 0.0 sort.19.cloned.1.call-start
  107.2 0.6 copy-done.2
  107.7 0.2 select_reduce_fusion.2
  107.9 0.6 gather_fusion.2
  108.6 0.0 copy-done
  108.6 0.6 gather_fusion
  109.2 0.7 broadcast_select_fusion
  109.8 0.6 iota.37
  110.4 0.0 sort.19.cloned.1.call-update
  110.4 0.2 reduce-scatter.2.cloned.1.call-start
  110.7 266.6 %all-reduce.2.cloned.1.call-done = f32[2048,1024]{1,0:T(8,128)} async-done(((f32[2048,1024]{1,0:T(8,128)}), f32[2048,1024]{1,0:T(8,128)}) %all-reduce.2.cloned.1.call-update) | async-done | bytes 8388624 | tf_op jit(solution)/shard_map/psum | solution.py:50
  377.3 31.6 %convolution_bitcast_fusion = f32[1024,1024]{0,1:T(8,128)} fusion(f32[2048,1024]{1,0:T(8,128)} %all-reduce.2.cloned.1.call-done, f32[2048,1024]{1,0:T(8,128)} %param.8), kind=kOutput, calls=%fused_computation.10 | convolution fusion | flops 25769803776 | bytes 20971520 | tf_op jit(solution)/shard_map/dot_general | solution.py:51
  408.9 0.0 reduce-scatter.2.cloned.1.call-update
  409.0 0.1 select_reduce_fusion.1
  409.1 0.1 convert_reduce_fusion
  409.2 0.0 sort.19.cloned.1.call-done
  409.2 0.7 fusion.1
  409.9 0.7 compare_and_fusion.1
  410.6 42.2 %reduce-scatter.2.cloned.1.call-done = f32[1024,256]{0,1:T(8,128)} async-done(((f32[1024,1024]{0,1:T(8,128)}), f32[1024,256]{0,1:T(8,128)}) %reduce-scatter.2.cloned.1.call-update) | async-done | bytes 1048592 | tf_op jit(solution)/shard_map/reduce_scatter | solution.py:58
  452.8 1.6 copy.11
  454.3 7.3 %gather_fusion.6 = f32[1024,256]{1,0:T(8,128)S(1)} fusion(f32[4,256,256]{2,1,0:T(8,128)S(1)} %bitcast.40, s32[1024]{0:T(1024)S(1)} %bitcast.41), kind=kCustom, calls=%fused_computation.6 | custom fusion | bytes 2105344 | tf_op jit(solution)/shard_map/vmap(jit(_take))/gather | solution.py:8
  461.6 0.2 select_multiply_fusion.2
  461.9 0.0 copy-start.3
  461.9 0.7 gather_fusion.3
  462.6 0.0 copy-start.1
  462.6 1.6 select_multiply_fusion.1
  464.2 5.5 %all-to-all-start = ((f32[8,256,256]{2,1,0:T(8,128)}), f32[8,256,256]{2,1,0:T(8,128)S(1)}, u32[]{:S(2)}, u32[]{:S(2)}) async-start(f32[8,256,256]{2,1,0:T(8,128)} %select_multiply_fusion.1), calls=%async_computation.1 | async-start | bytes 4194304 | tf_op jit(solution)/shard_map/all_to_all | solution.py:69
  469.7 0.6 dynamic-slice.2
  471.0 0.1 compare_and_fusion.5
  471.1 46.7 %all-to-all-done = f32[8,256,256]{2,1,0:T(8,128)S(1)} async-done(((f32[8,256,256]{2,1,0:T(8,128)}), f32[8,256,256]{2,1,0:T(8,128)S(1)}, u32[]{:S(2)}, u32[]{:S(2)}) %all-to-all-start) | async-done | bytes 2097184 | tf_op jit(solution)/shard_map/all_to_all | solution.py:69
  517.8 1.8 gather_fusion.4
  519.6 3.3 add_multiply_fusion
  (21 shorter events, 0.2 us)
Async XLA Ops:
  7.4 51.5 %all-gather.2.cloned.1.call-start = ((), (), s32[]{:S(2)}) async-start(), calls=%async_computation.2 | async-start | bytes 7864320 | tf_op jit(solution)/shard_map/all_gather | solution.py:42
  8.1 369.2 %all-reduce.2.cloned.1.call-start = ((), (), s32[]{:S(2)}) async-start(), calls=%async_computation.3 | async-start | bytes 16777216 | tf_op jit(solution)/shard_map/psum | solution.py:50
  107.1 0.7 copy-start.2
  107.1 1.5 copy-start
  107.1 302.1 %sort.19.cloned.1.call-start = ((), (), s32[]{:S(2)}) async-start(), calls=%async_computation.5 | async-start | bytes 24608 | tf_op jit(solution)/shard_map/jit(argsort)/sort | solution.py:60
  110.4 342.3 %reduce-scatter.2.cloned.1.call-start = ((), (), s32[]{:S(2)}) async-start(), calls=%async_computation.4 | async-start | bytes 5242880 | tf_op jit(solution)/shard_map/reduce_scatter | solution.py:58
  461.9 7.9 %copy-start.3 = (s32[8]{0:T(128)S(1)}, s32[8]{0:T(128)}, u32[]{:S(2)}) copy-start(s32[8]{0:T(128)} %param.9) | copy-start | bytes 100
  462.6 57.0 %copy-start.1 = (f32[6,256]{1,0:T(8,128)S(1)}, f32[6,256]{1,0:T(8,128)}, u32[]{:S(2)}) copy-start(f32[6,256]{1,0:T(8,128)} %param.13) | copy-start | bytes 18436
  464.2 53.6 %all-to-all-start = ((f32[8,256,256]{2,1,0:T(8,128)}), f32[8,256,256]{2,1,0:T(8,128)S(1)}, u32[]{:S(2)}, u32[]{:S(2)}) async-start(f32[8,256,256]{2,1,0:T(8,128)} %select_multiply_fusion.1), calls=%async_computation.1 | async-start | bytes 4194304 | tf_op jit(solution)/shard_map/all_to_all | solution.py:69
Sparse Core Ops, SparseCore 0:
  9.7 49.0 all-gather.1
  107.2 270.0 all-reduce.1
  409.1 43.6 reduce-scatter.1
Sparse Core Ops, SparseCore 1:
  110.5 2.5 sort.21.cloned.1.call-done
  (1 shorter events, 0.0 us)
where the time goes:
time: 531 us; the launch traced here: 530 us
  waiting for transfers between devices  404 us (76%)
  local copies, waits for them, and re-layouts  52.1 us (10%)
  matrix products  31.6 us (6%)
  other arithmetic  21.4 us (4%)
  between operations  15.3 us (3%)
  starting transfers between devices  5.77 us (1%)
    psum x1, waiting for transfers between devices, local(): lax.psum(placed.reshape(row_blocks * tile_rows, widened.shape[2]), 'col')  267 us
    all_gather x1, waiting for transfers between devices, local(): widened = lax.all_gather(amplitudes, 'row', axis=2, tiled=True)  47.4 us
    all_to_all x1, waiting for transfers between devices, local(): lax.all_to_all(outgoing, 'col', split_axis=0, concat_axis=0, tiled=True)  46.7 us
    reduce_scatter x1, waiting for transfers between devices, local(): lax.psum_scatter(partial_cols, 'row', scatter_dimension=1, tiled=True)  42.2 us
    gather x3, local copies, waits for them, and re-layouts, tile_recouple(): jnp.take(single, ordering, axis=0)  37.7 us
    dot_general x1, matrix products, local(): lax.dot_general(interaction, crossed, (((0,), (0,)), ((), ())), precision...  31.6 us
  transfers between devices with their start and end apart: 4, of which 4 were waited for; matrix products, arithmetic and copies ran while one was open for 2% of the time, Pallas kernels for 0%

commit v1 on v0

--- a/solution.py
+++ b/solution.py
@@ -47,7 +47,9 @@
     placed = (
         jnp.take(widened, group_tiles % slots, axis=0) * is_owned.astype(jnp.float32)[:, None, None]
     )
-    crossed = lax.psum(placed.reshape(row_blocks * tile_rows, widened.shape[2]), "col")
+    part = placed.reshape(row_blocks * tile_rows, widened.shape[2])
+    parts = lax.all_gather(part, "col", axis=0, tiled=False)
+    crossed = parts.sum(axis=0)
     partial_cols = lax.dot_general(
         interaction,
         crossed,

time: 531 us -> 1550 us (2.92)
  waiting for transfers between devices: 404 us -> 1400 us
  other arithmetic: 21.4 us -> 46 us
    all_gather x0 -> x1, waiting for transfers between devices: none -> 1260 us  [local(): parts = lax.all_gather(part, 'col', axis=0, tiled=False)]
    psum x1 -> x0, waiting for transfers between devices: 267 us -> none  [local(): lax.psum(placed.reshape(row_blocks * tile_rows, widened.shape[2]), 'col')]
    reduce_sum x0 -> x1, other arithmetic: none -> 24.5 us  [local(): crossed = parts.sum(axis=0)]
  transfers between devices with their start and end apart: 4 -> 4, of which waited for: 4 -> 4; matrix products, arithmetic and copies ran while one was open for 2% -> 1% of each run, Pallas kernels for 0% -> 0%
where the time goes in v1:
time: 1550 us
  waiting for transfers between devices  1400 us (90%)
  local copies, waits for them, and re-layouts  52.1 us (3%)
  other arithmetic  46 us (3%)
  matrix products  31.6 us (2%)
    all_gather x1, waiting for transfers between devices, local(): parts = lax.all_gather(part, 'col', axis=0, tiled=False)  1260 us
    all_gather x1, waiting for transfers between devices, local(): widened = lax.all_gather(amplitudes, 'row', axis=2, tiled=True)  47.4 us
    all_to_all x1, waiting for transfers between devices, local(): lax.all_to_all(outgoing, 'col', split_axis=0, concat_axis=0, tiled=True)  46.7 us
    reduce_scatter x1, waiting for transfers between devices, local(): lax.psum_scatter(partial_cols, 'row', scatter_dimension=1, tiled=True)  43.1 us
    gather x3, local copies, waits for them, and re-layouts, tile_recouple(): jnp.take(single, ordering, axis=0)  37.7 us
    dot_general x1, matrix products, local(): lax.dot_general(interaction, crossed, (((0,), (0,)), ((), ())), precision...  31.6 us
  transfers between devices with their start and end apart: 4, of which 4 were waited for; matrix products, arithmetic and copies ran while one was open for 1% of the time, Pallas kernels for 0%

profile of v1, /device:TPU:0, one launch (start us, length us, event | category | flops | bytes accessed | tf_op | source)
XLA Modules:
  0.0 1552.3 jit_solution(3391319183507431112)
XLA Ops:
  7.4 0.0 all-gather.3.cloned.1.call-start
  7.4 0.7 all-gather.3.cloned.1.call-update
  8.1 0.0 all-gather.5.cloned.1.call-start
  8.1 0.7 subtract_convert_fusion
  8.8 0.1 dynamic_slice.11
  8.9 0.7 bitcast_or_fusion
  9.6 0.8 select_reduce_fusion
  10.5 0.1 broadcast_bitcast_fusion
  10.6 0.1 broadcast_in_dim.144
  10.7 0.7 compare_and_fusion
  11.4 47.4 %all-gather.3.cloned.1.call-done = f32[6,256,1024]{2,1,0:T(8,128)} async-done(((f32[6,256,256]{2,1,0:T(8,128)}), f32[6,256,1024]{2,1,0:T(8,128)}) %all-gather.3.cloned.1.call-update) | async-done | bytes 6291472 | tf_op jit(solution)/shard_map/all_gather | solution.py:42
  58.8 30.4 %gather_fusion.5 = f32[1536,1024]{1,0:T(8,128)} fusion(f32[6,256,1024]{2,1,0:T(8,128)} %all-gather.3.cloned.1.call-done, s32[1536]{0:T(1024)S(1)} %reshape.270), kind=kCustom, calls=%fused_computation.5 | custom fusion | bytes 12595200 | tf_op jit(solution)/shard_map/vmap(jit(_take))/gather | solution.py:8
  89.3 4.9 select_multiply_fusion
  94.2 7.1 gather_fusion.1
  101.2 5.8 fusion
  107.0 0.0 all-gather.5.cloned.1.call-update
  107.1 0.0 sort.19.cloned.1.call-start
  107.1 0.6 copy-done.2
  107.7 0.2 select_reduce_fusion.2
  107.9 0.6 gather_fusion.2
  108.5 0.6 gather_fusion
  109.1 0.7 broadcast_select_fusion
  109.8 0.6 iota.37
  110.4 0.0 sort.19.cloned.1.call-update
  110.4 0.2 reduce-scatter.2.cloned.1.call-start
  110.6 1263.5 %all-gather.5.cloned.1.call-done = f32[8,2048,1024]{2,1,0:T(8,128)} async-done(((f32[1,2048,1024]{2,1,0:T(8,128)}), f32[8,2048,1024]{2,1,0:T(8,128)}) %all-gather.5.cloned.1.call-update) | async-done | bytes 67108880 | tf_op jit(solution)/shard_map/all_gather | solution.py:51
  1374.1 24.5 %reduce_sum.44 = f32[2048,1024]{1,0:T(8,128)} reduce(f32[8,2048,1024]{2,1,0:T(8,128)} %all-gather.5.cloned.1.call-done, f32[]{:T(128)} %constant.163.clone.1), dimensions={0}, to_apply=%region_4.5 | reduce | flops 14680064 | bytes 75497472 | tf_op jit(solution)/shard_map/reduce_sum | solution.py:52
  1398.6 31.6 %convolution_bitcast_fusion = f32[1024,1024]{0,1:T(8,128)} fusion(f32[2048,1024]{1,0:T(8,128)} %reduce_sum.44, f32[2048,1024]{1,0:T(8,128)} %param.8), kind=kOutput, calls=%fused_computation.10 | convolution fusion | flops 25769803776 | bytes 20971520 | tf_op jit(solution)/shard_map/dot_general | solution.py:53
  1430.3 0.0 reduce-scatter.2.cloned.1.call-update
  1430.3 0.1 select_reduce_fusion.1
  1430.4 0.1 convert_reduce_fusion
  1430.5 0.0 sort.19.cloned.1.call-done
  1430.5 0.7 fusion.1
  1431.2 0.7 compare_and_fusion.1
  1431.9 43.1 %reduce-scatter.2.cloned.1.call-done = f32[1024,256]{0,1:T(8,128)} async-done(((f32[1024,1024]{0,1:T(8,128)}), f32[1024,256]{0,1:T(8,128)}) %reduce-scatter.2.cloned.1.call-update) | async-done | bytes 1048592 | tf_op jit(solution)/shard_map/reduce_scatter | solution.py:60
  1475.0 1.6 copy.12
  1476.6 7.3 gather_fusion.6
  1483.9 0.2 select_multiply_fusion.2
  1484.1 0.0 copy-start.3
  1484.1 0.7 gather_fusion.3
  1484.8 0.0 copy-start.1
  1484.8 1.6 select_multiply_fusion.1
  1486.5 5.5 all-to-all-start
  1492.0 0.6 dynamic-slice.2
  1493.2 0.1 compare_and_fusion.5
  1493.3 46.7 %all-to-all-done = f32[8,256,256]{2,1,0:T(8,128)S(1)} async-done(((f32[8,256,256]{2,1,0:T(8,128)}), f32[8,256,256]{2,1,0:T(8,128)S(1)}, u32[]{:S(2)}, u32[]{:S(2)}) %all-to-all-start) | async-done | bytes 2097184 | tf_op jit(solution)/shard_map/all_to_all | solution.py:71
  1540.0 1.8 gather_fusion.4
  1541.8 3.3 add_multiply_fusion
  (22 shorter events, 0.2 us)
Async XLA Ops:
  7.4 51.5 %all-gather.3.cloned.1.call-start = ((), (), s32[]{:S(2)}) async-start(), calls=%async_computation.2 | async-start | bytes 7864320 | tf_op jit(solution)/shard_map/all_gather | solution.py:42
  8.1 1366.0 %all-gather.5.cloned.1.call-start = ((), (), s32[]{:S(2)}) async-start(), calls=%async_computation.3 | async-start | bytes 75497472 | tf_op jit(solution)/shard_map/all_gather | solution.py:51
  107.0 0.7 copy-start.2
  107.0 1.5 copy-start
  107.1 1323.4 %sort.19.cloned.1.call-start = ((), (), s32[]{:S(2)}) async-start(), calls=%async_computation.5 | async-start | bytes 24608 | tf_op jit(solution)/shard_map/jit(argsort)/sort | solution.py:62
  110.4 1364.6 %reduce-scatter.2.cloned.1.call-start = ((), (), s32[]{:S(2)}) async-start(), calls=%async_computation.4 | async-start | bytes 5242880 | tf_op jit(solution)/shard_map/reduce_scatter | solution.py:60
  1484.1 7.9 copy-start.3
  1484.8 57.0 %copy-start.1 = (f32[6,256]{1,0:T(8,128)S(1)}, f32[6,256]{1,0:T(8,128)}, u32[]{:S(2)}) copy-start(f32[6,256]{1,0:T(8,128)} %param.13) | copy-start | bytes 18436
  1486.5 53.6 %all-to-all-start = ((f32[8,256,256]{2,1,0:T(8,128)}), f32[8,256,256]{2,1,0:T(8,128)S(1)}, u32[]{:S(2)}, u32[]{:S(2)}) async-start(f32[8,256,256]{2,1,0:T(8,128)} %select_multiply_fusion.1), calls=%async_computation.1 | async-start | bytes 4194304 | tf_op jit(solution)/shard_map/all_to_all | solution.py:71
Sparse Core Ops, SparseCore 0:
  9.7 49.0 all-gather.2
  107.2 1266.8 all-gather.4
  1430.4 44.5 reduce-scatter.1
Sparse Core Ops, SparseCore 1:
  110.5 2.5 sort.21.cloned.1.call-done
  (1 shorter events, 0.0 us)
